TPU v7x, 32 devices: a whole 2x2x4 slice. The times are simulated.
32 devices in a mesh: seq: 4 (over y, x), fsdp: 8 (over z, core).
Axes of the slice: x: 2, y: 2, z: 4, core: 2. Of those that a mesh axis runs over, the one named last changes fastest.
Arguments:
- tokens: bfloat16 [8, 512, 8192], P('fsdp', 'seq'), may hold values from -6 to 6
- norm_gain: float32 [8192], replicated, may hold values from 0.3 to 3
- w_query: bfloat16 [8192, 4096], P(('seq', 'fsdp')), may hold values from -1 to 1
- key_weight: bfloat16 [8192, 512], P(('seq', 'fsdp')), may hold values from -1 to 1
- value_weight: bfloat16 [8192, 512], P(('seq', 'fsdp')), may hold values from -0.0625 to 0.0625
- w_out: bfloat16 [4096, 8192], P(None, ('seq', 'fsdp')), may hold values from -0.09375 to 0.09375
Outputs:
- result: float32 [8, 512, 8192], P('fsdp', 'seq')
All inputs are finite; a program needn't handle non-finite values.
Results may differ from a plain program's by a relative error of at most 0.04.
Values may be sent and summed in bfloat16 or wider, within the bound.
A program may use at most 128 MiB of HBM per device.

v0:
```python
import jax
import jax.numpy as jnp
from jax import lax
from jax.sharding import PartitionSpec as P

HEAD_SIZE = 128


def body(tokens, norm_gain, w_query, key_weight, value_weight, w_out):
    floats = tokens[0].astype(jnp.float32)
    mean_square = jnp.mean(floats * floats, axis=-1, keepdims=True)
    normed_input = (floats * lax.rsqrt(mean_square + 1e-05) * norm_gain).astype(jnp.bfloat16)
    spread = lax.all_to_all(normed_input[None], "seq", split_axis=2, concat_axis=1, tiled=True)[0]
    seq_length = spread.shape[0]
    group_size = lax.axis_size("seq")
    device_index = lax.axis_index("seq")
    query_heads = w_query.shape[1] // HEAD_SIZE
    key_heads = key_weight.shape[1] // HEAD_SIZE
    group_width = query_heads // key_heads
    local_heads = query_heads // group_size
    portions = (
        lax.all_gather(w_query, "fsdp", axis=0, tiled=True),
        lax.all_gather(key_weight, "fsdp", axis=0, tiled=True),
        lax.all_gather(value_weight, "fsdp", axis=0, tiled=True),
    )
    query_part, key_part, value_part = tuple(
        (jnp.dot(spread, portion, preferred_element_type=jnp.float32) for portion in portions)
    )
    query_sum = lax.psum_scatter(
        query_part.astype(jnp.bfloat16), "seq", scatter_dimension=1, tiled=True
    )
    key_all, value_all = (
        lax.psum(key_part.astype(jnp.bfloat16), "seq").astype(jnp.float32),
        lax.psum(value_part.astype(jnp.bfloat16), "seq").astype(jnp.float32),
    )
    offset = device_index * local_heads // group_width * HEAD_SIZE
    key_rows = lax.dynamic_slice_in_dim(key_all, offset, HEAD_SIZE, 1).astype(jnp.bfloat16)
    value_rows = lax.dynamic_slice_in_dim(value_all, offset, HEAD_SIZE, 1).astype(jnp.bfloat16)
    queries = jnp.transpose(query_sum.reshape(seq_length, local_heads, HEAD_SIZE), (1, 0, 2))
    scale = HEAD_SIZE ** (-0.5)
    row_ids = lax.broadcasted_iota(jnp.int32, (seq_length, seq_length), 0)
    col_ids = lax.broadcasted_iota(jnp.int32, (seq_length, seq_length), 1)
    causal = row_ids >= col_ids

    def one_head(query_head):
        scores = (
            jnp.einsum("qd,kd->qk", query_head, key_rows, preferred_element_type=jnp.float32)
            * scale
        )
        scores = jnp.where(causal, scores, jnp.float32(-1e30))
        top = jnp.max(scores, axis=-1, keepdims=True)
        weights = jnp.exp(scores - top)
        probs = (weights / jnp.sum(weights, axis=-1, keepdims=True)).astype(jnp.bfloat16)
        return jnp.dot(probs, value_rows, preferred_element_type=jnp.float32).astype(jnp.bfloat16)

    attended = lax.map(one_head, queries)
    heads_out = jnp.transpose(attended, (1, 0, 2)).reshape(seq_length, local_heads * HEAD_SIZE)
    out_columns = lax.all_gather(w_out, "fsdp", axis=1, tiled=True)
    mixed = jnp.dot(
        lax.all_gather(heads_out, "seq", axis=1, tiled=True),
        out_columns,
        preferred_element_type=jnp.float32,
    )
    branch = mixed.astype(jnp.bfloat16)
    returned = lax.all_to_all(branch[None], "seq", split_axis=1, concat_axis=2, tiled=True)
    return tokens.astype(jnp.float32) + returned.astype(jnp.float32)


def solution(mesh):
    placed = (
        P("fsdp", "seq", None),
        P(),
        P(("seq", "fsdp"), None),
        P(("seq", "fsdp"), None),
        P(("seq", "fsdp"), None),
        P(None, ("seq", "fsdp")),
    )
    return jax.shard_map(
        body, mesh=mesh, in_specs=placed, out_specs=P("fsdp", "seq", None), check_vma=False
    )
```

profile of v0, /device:TPU:0, one launch (start us, length us, event | category | flops | bytes accessed | tf_op | source)
XLA Modules:
  0.0 635.2 jit_solution(5943152748968882074)
XLA Ops:
  6.5 0.7 all-gather.10.cloned.1.call-update
  7.3 0.7 all-gather.8.cloned.1.call-update
  8.1 0.7 all-gather.6.cloned.1.call-update
  8.8 0.5 fusion.8
  9.3 1.9 fusion.10
  11.2 9.5 %copy.25 = bf16[1,128,8192]{1,0,2:T(2,128)(2,1)} copy(bf16[1,128,8192]{2,1,0:T(8,128)(2,1)} %fusion.10) | data formatting | bytes 4194304 | tf_op jit(solution)/shard_map/convert_element_type | solution.py:12
  20.7 0.6 broadcast.27
  21.3 46.5 %reduce.1 = bf16[8192,128]{1,0:T(8,128)(2,1)} reduce(bf16[8192,1,128]{2,1,0:T(2,128)(2,1)} %bitcast.52, bf16[]{:T(256)} %broadcast.27), dimensions={1}, to_apply=%bitcast.23.reduce_sub_computation | reduce | bytes 4194306
  67.8 4.0 reshape.53
  71.8 31.4 %all_to_all.24 = bf16[4,2,131072]{2,1,0:T(2,128)(2,1)} all-to-all(bf16[4,2,131072]{2,1,0:T(2,128)(2,1)} %reshape.53), channel_id=1, replica_groups=mesh['seq'=4,'fsdp'=8] {'seq'}, dimensions={0} | all-to-all | bytes 4194304 | tf_op jit(solution)/shard_map/all_to_all | solution.py:13
  103.2 4.9 reshape.54
  108.2 3.9 copy.33
  112.0 4.0 copy.26
  116.0 4.3 convolution_convert_fusion.3
  120.3 4.4 convolution_convert_fusion.4
  124.7 0.2 reduce-scatter.2.cloned.1.call-start
  125.0 98.2 %all-gather.6.cloned.1.call-done = bf16[2048,4096]{1,0:T(8,128)(2,1)} async-done(((bf16[256,4096]{1,0:T(8,128)(2,1)}), bf16[2048,4096]{1,0:T(8,128)(2,1)}) %all-gather.6.cloned.1.call-update) | async-done | bytes 16777232 | tf_op jit(solution)/shard_map/all_gather | solution.py:22
  223.1 14.3 %convolution_convert_fusion.1 = bf16[512,4096]{1,0:T(8,128)(2,1)} fusion(bf16[512,2048]{1,0:T(8,128)(2,1)} %bitcast.60, bf16[2048,4096]{1,0:T(8,128)(2,1)} %all-gather.6.cloned.1.call-done), kind=kOutput, calls=%fused_computation.16 | convolution fusion | flops 8592031744 | bytes 23068672 | tf_op jit(solution)/shard_map/dot_general | solution.py:27
  237.5 0.5 all-gather.14.cloned.1.call-update
  238.1 38.6 %all-reduce.3.cloned.1.call-done = (bf16[512,512]{1,0:T(8,128)(2,1)}, bf16[512,512]{1,0:T(8,128)(2,1)}) async-done(((bf16[512,512]{1,0:T(8,128)(2,1)}, bf16[512,512]{1,0:T(8,128)(2,1)}), (bf16[512,512]{1,0:T(8,128)(2,1)}, bf16[512,512]{1,0:T(8,128)(2,1)})) %all-reduce.3.cloned.1.call-update) | async-done | bytes 1048592 | tf_op jit(solution)/shard_map/psum | solution.py:33
  276.8 1.6 convert_convert_fusion
  278.4 53.8 %reduce-scatter.2.cloned.1.call-done = bf16[512,1024]{1,0:T(8,128)(2,1)} async-done(((bf16[512,4096]{1,0:T(8,128)(2,1)}), bf16[512,1024]{1,0:T(8,128)(2,1)}) %reduce-scatter.2.cloned.1.call-update) | async-done | bytes 1048592 | tf_op jit(solution)/shard_map/reduce_scatter | solution.py:29
  332.2 2.4 bitcast_bitcast_fusion
  334.6 16.4 %while.11 = (s32[]{:T(128)}, bf16[8,512,128]{1,2,0:T(8,128)(2,1)S(1)}, bf16[8,512,128]{2,1,0:T(8,128)(2,1)}, bf16[512,128]{1,0:T(8,128)(2,1)}, bf16[512,128]{1,0:T(8,128)(2,1)S(1)}, /*index=5*/s32[]{:T(128)}) while((s32[]{:T(128)}, bf16[8,512,128]{1,2,0:T(8,128)(2,1)S(1)}, bf16[8,512,128]{2,1,0:T(8,128)(2,1)}, ...), condition=%wide.region_7.8_spmd.clone, body=%wide.region_4.7_spmd.clone.sunk | while | flops 136641536 | bytes 4205129 | solution.py:56
  334.6 1.3 fusion.31
  335.8 0.2 fusion.32
  336.0 0.4 fusion.33
  336.6 1.3 fusion.31
  337.9 0.2 fusion.32
  338.1 0.4 fusion.33
  338.5 0.1 copy.41
  338.6 1.3 fusion.31
  339.9 0.2 fusion.32
  340.1 0.4 fusion.33
  340.5 0.1 copy.41
  340.6 1.3 fusion.31
  342.0 0.2 fusion.32
  342.2 0.4 fusion.33
  342.6 0.1 copy.41
  342.7 1.3 fusion.31
  344.0 0.2 fusion.32
  344.2 0.4 fusion.33
  344.8 1.3 fusion.31
  346.1 0.2 fusion.32
  346.3 0.4 fusion.33
  346.7 0.1 copy.41
  346.9 1.3 fusion.31
  348.2 0.2 fusion.32
  348.4 0.4 fusion.33
  348.9 1.3 fusion.31
  350.2 0.2 fusion.32
  350.4 0.4 fusion.33
  350.9 1.0 copy-done.1
  351.9 133.5 %all-gather.14.cloned.1.call-done = bf16[4096,2048]{1,0:T(8,128)(2,1)} async-done(((bf16[4096,256]{1,0:T(8,128)(2,1)}), bf16[4096,2048]{1,0:T(8,128)(2,1)}) %all-gather.14.cloned.1.call-update) | async-done | bytes 16777232 | tf_op jit(solution)/shard_map/all_gather | solution.py:58
  485.5 52.6 %all-gather.12.cloned.1.call-done = bf16[512,4096]{0,1:T(8,128)(2,1)} async-done(((bf16[512,1024]{0,1:T(8,128)(2,1)}), bf16[512,4096]{0,1:T(8,128)(2,1)}) %all-gather.12.cloned.1.call-update) | async-done | bytes 4194320 | tf_op jit(solution)/shard_map/all_gather | solution.py:60
  538.1 13.6 %fusion.11 = bf16[1,512,2048]{2,1,0:T(8,128)(2,1)S(1)} fusion(bf16[512,4096]{0,1:T(8,128)(2,1)} %all-gather.12.cloned.1.call-done, bf16[4096,2048]{1,0:T(8,128)(2,1)} %all-gather.14.cloned.1.call-done), kind=kOutput, calls=%fused_computation.22 | convolution fusion | flops 8590983168 | bytes 23068672 | tf_op jit(solution)/shard_map/dot_general | solution.py:59
  551.7 5.2 copy.39
  557.0 14.5 %reduce.2 = bf16[512,2048]{1,0:T(8,128)(2,1)} reduce(bf16[512,1,2048]{2,1,0:T(2,128)(2,1)} %bitcast.53, bf16[]{:T(256)} %broadcast.27), dimensions={1}, to_apply=%bitcast.43.reduce_sub_computation | reduce | bytes 4194306
  571.5 4.5 reshape.55
  576.0 29.9 %all_to_all.25 = bf16[4,2,131072]{2,1,0:T(2,128)(2,1)} all-to-all(bf16[4,2,131072]{2,1,0:T(2,128)(2,1)} %reshape.55), channel_id=1, replica_groups=mesh['seq'=4,'fsdp'=8] {'seq'}, dimensions={0} | all-to-all | bytes 4194304 | tf_op jit(solution)/shard_map/all_to_all | solution.py:65
  605.9 4.9 reshape.56
  610.9 6.8 %copy.38 = f32[1,4,128,2048]{3,1,2,0:T(4,128)} copy(bf16[1,4,128,2048]{3,0,2,1:T(2,128)(2,1)} %bitcast.55) | data formatting | bytes 6291456 | tf_op jit(solution)/shard_map/convert_element_type | solution.py:66
  617.7 6.0 reshape.51
  623.7 4.6 convert_add_fusion
  (30 shorter events, 0.9 us)
Async XLA Ops:
  6.5 2.3 copy-start
  6.5 109.5 %all-gather.10.cloned.1.call-start = ((), (), s32[]{:S(2)}) async-start(), calls=%async_computation.6 | async-start | bytes 2359296 | tf_op jit(solution)/shard_map/all_gather | solution.py:24
  7.3 113.0 %all-gather.8.cloned.1.call-start = ((), (), s32[]{:S(2)}) async-start(), calls=%async_computation.5 | async-start | bytes 2359296 | tf_op jit(solution)/shard_map/all_gather | solution.py:23
  8.0 1.3 copy-start.2
  8.0 215.1 %all-gather.6.cloned.1.call-start = ((), (), s32[]{:S(2)}) async-start(), calls=%async_computation.3 | async-start | bytes 18874368 | tf_op jit(solution)/shard_map/all_gather | solution.py:22
  8.8 268.0 %all-reduce.3.cloned.1.call-start = ((), (), s32[]{:S(2)}) async-start(), calls=%async_computation.9 | async-start | bytes 2097152 | tf_op jit(solution)/shard_map/psum | solution.py:33
  124.7 207.4 %reduce-scatter.2.cloned.1.call-start = ((), (), s32[]{:S(2)}) async-start(), calls=%async_computation.4 | async-start | bytes 5242880 | tf_op jit(solution)/shard_map/reduce_scatter | solution.py:29
  237.5 248.0 %all-gather.14.cloned.1.call-start = ((), (), s32[]{:S(2)}) async-start(), calls=%async_computation.8 | async-start | bytes 18874368 | tf_op jit(solution)/shard_map/all_gather | solution.py:58
  238.0 300.0 %all-gather.12.cloned.1.call-start = ((), (), s32[]{:S(2)}) async-start(), calls=%async_computation.7 | async-start | bytes 5242880 | tf_op jit(solution)/shard_map/all_gather | solution.py:60
  350.9 1.0 copy-start.1
Sparse Core Ops, SparseCore 0:
  8.9 31.8 all-gather.9
  42.4 28.5 all-gather.7
  72.6 150.4 all-gather.5
  226.0 50.6 all-reduce.2
  279.6 52.5 reduce-scatter.1
  333.6 151.7 all-gather.13
  487.3 50.7 all-gather.11
where the time goes:
time: 636 us; the launch traced here: 635 us
  waiting for transfers between devices  379 us (60%)
  other arithmetic  71.3 us (11%)
  blocking collectives  61.3 us (10%)
  local copies, waits for them, and re-layouts  58.8 us (9%)
  matrix products  50.1 us (8%)
  between operations  13.6 us (2%)
    all_gather x1, waiting for transfers between devices, body(): out_columns = lax.all_gather(w_out, 'fsdp', axis=1, tiled=True)  134 us
    all_gather x1, waiting for transfers between devices, body(): lax.all_gather(w_query, 'fsdp', axis=0, tiled=True)  98.2 us
    unnamed x2, other arithmetic  61.1 us
    reduce_scatter x1, waiting for transfers between devices, body(): lax.psum_scatter(query_part.astype(jnp.bfloat16), 'seq', scatter_dimensio...  53.8 us
    all_gather x1, waiting for transfers between devices, body(): lax.all_gather(heads_out, 'seq', axis=1, tiled=True)  52.6 us
    psum x1, waiting for transfers between devices, body(): lax.psum(key_part.astype(jnp.bfloat16), 'seq').astype(jnp.float32)  38.6 us
    all_to_all x1, blocking collectives, body(): lax.all_to_all(normed_input[None], 'seq', split_axis=2, concat_axis=1, ti...  31.4 us
    all_to_all x1, blocking collectives, body(): lax.all_to_all(branch[None], 'seq', split_axis=1, concat_axis=2, tiled=True)  29.9 us
  transfers between devices with their start and end apart: 7, of which 5 were waited for; matrix products, arithmetic and copies ran while one was open for 19% of the time, Pallas kernels for 0%

commit v1 on v0

--- a/solution.py
+++ b/solution.py
@@ -4,6 +4,12 @@
 from jax.sharding import PartitionSpec as P
 
 HEAD_SIZE = 128
+
+
+def gather_and_add(block, axis):
+    parts = lax.all_gather(block, axis, axis=0, tiled=False)
+    total = parts.sum(axis=0)
+    return total
 
 
 def body(tokens, norm_gain, w_query, key_weight, value_weight, w_out):
@@ -30,7 +36,7 @@
         query_part.astype(jnp.bfloat16), "seq", scatter_dimension=1, tiled=True
     )
     key_all, value_all = (
-        lax.psum(key_part.astype(jnp.bfloat16), "seq").astype(jnp.float32),
+        gather_and_add(key_part.astype(jnp.bfloat16), "seq").astype(jnp.float32),
         lax.psum(value_part.astype(jnp.bfloat16), "seq").astype(jnp.float32),
     )
     offset = device_index * local_heads // group_width * HEAD_SIZE

time: 636 us -> 666 us (1.047)
  waiting for transfers between devices: 379 us -> 406 us
    all_gather x0 -> x1, waiting for transfers between devices: none -> 36 us  [gather_and_add(): parts = lax.all_gather(block, axis, axis=0, tiled=False)]
    psum x1, waiting for transfers between devices: 38.6 us -> 31.3 us  [body(): lax.psum(value_part.astype(jnp.bfloat16), 'seq').astype(jnp.float32)]
  transfers between devices with their start and end apart: 7 -> 8, of which waited for: 5 -> 6; matrix products, arithmetic and copies ran while one was open for 19% -> 18% of each run, Pallas kernels for 0% -> 0%
where the time goes in v1:
time: 666 us; the launch traced here: 665 us
  waiting for transfers between devices  406 us (61%)
  other arithmetic  74.9 us (11%)
  blocking collectives  61.3 us (9%)
  local copies, waits for them, and re-layouts  58.8 us (9%)
  matrix products  50.1 us (8%)
  between operations  13.6 us (2%)
    all_gather x1, waiting for transfers between devices, body(): out_columns = lax.all_gather(w_out, 'fsdp', axis=1, tiled=True)  134 us
    all_gather x1, waiting for transfers between devices, body(): lax.all_gather(w_query, 'fsdp', axis=0, tiled=True)  98.2 us
    unnamed x2, other arithmetic  61 us
    all_gather x1, waiting for transfers between devices, body(): lax.all_gather(heads_out, 'seq', axis=1, tiled=True)  52.6 us
    reduce_scatter x1, waiting for transfers between devices, body(): lax.psum_scatter(query_part.astype(jnp.bfloat16), 'seq', scatter_dimensio...  51 us
    all_gather x1, waiting for transfers between devices, gather_and_add(): parts = lax.all_gather(block, axis, axis=0, tiled=False)  36 us
    all_to_all x1, blocking collectives, body(): lax.all_to_all(normed_input[None], 'seq', split_axis=2, concat_axis=1, ti...  31.4 us
    psum x1, waiting for transfers between devices, body(): lax.psum(value_part.astype(jnp.bfloat16), 'seq').astype(jnp.float32)  31.3 us
  transfers between devices with their start and end apart: 8, of which 6 were waited for; matrix products, arithmetic and copies ran while one was open for 18% of the time, Pallas kernels for 0%

profile of v1, /device:TPU:0, one launch (start us, length us, event | category | flops | bytes accessed | tf_op | source)
XLA Modules:
  0.0 665.0 jit_solution(14773272825732324825)
XLA Ops:
  6.5 0.7 all-gather.12.cloned.1.call-update
  7.3 0.7 all-gather.10.cloned.1.call-update
  8.1 0.7 all-gather.8.cloned.1.call-update
  8.8 0.5 fusion.8
  9.3 1.9 fusion.10
  11.2 9.5 %copy.25 = bf16[1,128,8192]{1,0,2:T(2,128)(2,1)} copy(bf16[1,128,8192]{2,1,0:T(8,128)(2,1)} %fusion.10) | data formatting | bytes 4194304 | tf_op jit(solution)/shard_map/convert_element_type | solution.py:18
  20.7 0.5 broadcast.27
  21.3 46.5 %reduce.2 = bf16[8192,128]{1,0:T(8,128)(2,1)} reduce(bf16[8192,1,128]{2,1,0:T(2,128)(2,1)} %bitcast.53, bf16[]{:T(256)} %broadcast.27), dimensions={1}, to_apply=%bitcast.24.reduce_sub_computation | reduce | bytes 4194306
  67.7 4.0 reshape.54
  71.7 31.4 %all_to_all.24 = bf16[4,2,131072]{2,1,0:T(2,128)(2,1)} all-to-all(bf16[4,2,131072]{2,1,0:T(2,128)(2,1)} %reshape.54), channel_id=1, replica_groups=mesh['seq'=4,'fsdp'=8] {'seq'}, dimensions={0} | all-to-all | bytes 4194304 | tf_op jit(solution)/shard_map/all_to_all | solution.py:19
  103.1 4.9 reshape.55
  108.1 3.8 copy.33
  111.9 4.0 copy.26
  115.9 4.3 convolution_convert_fusion.3
  120.3 4.4 convolution_convert_fusion.4
  124.7 0.2 reduce-scatter.2.cloned.1.call-start
  125.0 98.2 %all-gather.8.cloned.1.call-done = bf16[2048,4096]{1,0:T(8,128)(2,1)} async-done(((bf16[256,4096]{1,0:T(8,128)(2,1)}), bf16[2048,4096]{1,0:T(8,128)(2,1)}) %all-gather.8.cloned.1.call-update) | async-done | bytes 16777232 | tf_op jit(solution)/shard_map/all_gather | solution.py:28
  223.1 14.3 %convolution_convert_fusion.1 = bf16[512,4096]{1,0:T(8,128)(2,1)} fusion(bf16[512,2048]{1,0:T(8,128)(2,1)} %bitcast.62, bf16[2048,4096]{1,0:T(8,128)(2,1)} %all-gather.8.cloned.1.call-done), kind=kOutput, calls=%fused_computation.16 | convolution fusion | flops 8592031744 | bytes 23068672 | tf_op jit(solution)/shard_map/dot_general | solution.py:33
  237.5 0.7 all-gather.16.cloned.1.call-update
  238.3 31.3 %all-reduce.2.cloned.1.call-done = bf16[512,512]{1,0:T(8,128)(2,1)} async-done(((bf16[512,512]{1,0:T(8,128)(2,1)}), bf16[512,512]{1,0:T(8,128)(2,1)}) %all-reduce.2.cloned.1.call-update) | async-done | bytes 524304 | tf_op jit(solution)/shard_map/psum | solution.py:40
  269.6 0.9 convert_convert_fusion
  270.5 36.0 %all-gather.18.cloned.1.call-done = bf16[2048,512]{1,0:T(8,128)(2,1)} async-done(((bf16[512,512]{1,0:T(8,128)(2,1)}), bf16[2048,512]{1,0:T(8,128)(2,1)}) %all-gather.18.cloned.1.call-update) | async-done | bytes 2097168 | tf_op jit(solution)/shard_map/all_gather | solution.py:10
  306.5 2.8 reduce_sum.31
  309.3 1.6 convert_convert_fusion.1
  310.9 51.0 %reduce-scatter.2.cloned.1.call-done = bf16[512,1024]{1,0:T(8,128)(2,1)} async-done(((bf16[512,4096]{1,0:T(8,128)(2,1)}), bf16[512,1024]{1,0:T(8,128)(2,1)}) %reduce-scatter.2.cloned.1.call-update) | async-done | bytes 1048592 | tf_op jit(solution)/shard_map/reduce_scatter | solution.py:35
  361.9 2.4 bitcast_bitcast_fusion
  364.3 16.4 %while.11 = (s32[]{:T(128)}, bf16[8,512,128]{1,2,0:T(8,128)(2,1)S(1)}, bf16[8,512,128]{2,1,0:T(8,128)(2,1)}, bf16[512,128]{1,0:T(8,128)(2,1)}, bf16[512,128]{1,0:T(8,128)(2,1)S(1)}, /*index=5*/s32[]{:T(128)}) while((s32[]{:T(128)}, bf16[8,512,128]{1,2,0:T(8,128)(2,1)S(1)}, bf16[8,512,128]{2,1,0:T(8,128)(2,1)}, ...), condition=%wide.region_7.8_spmd.clone, body=%wide.region_4.7_spmd.clone.sunk | while | flops 136641536 | bytes 4205129 | solution.py:62
  364.3 1.3 fusion.31
  365.6 0.2 fusion.32
  365.8 0.4 fusion.33
  366.2 0.1 copy.42
  366.3 1.3 fusion.31
  367.6 0.2 fusion.32
  367.8 0.4 fusion.33
  368.4 1.3 fusion.31
  369.6 0.2 fusion.32
  369.8 0.4 fusion.33
  370.4 1.3 fusion.31
  371.7 0.2 fusion.32
  371.9 0.4 fusion.33
  372.5 1.3 fusion.31
  373.8 0.2 fusion.32
  374.0 0.4 fusion.33
  374.5 1.3 fusion.31
  375.9 0.2 fusion.32
  376.1 0.4 fusion.33
  376.6 1.3 fusion.31
  377.9 0.2 fusion.32
  378.1 0.4 fusion.33
  378.7 1.3 fusion.31
  379.9 0.2 fusion.32
  380.1 0.4 fusion.33
  380.7 1.0 copy-done.1
  381.7 133.6 %all-gather.16.cloned.1.call-done = bf16[4096,2048]{1,0:T(8,128)(2,1)} async-done(((bf16[4096,256]{1,0:T(8,128)(2,1)}), bf16[4096,2048]{1,0:T(8,128)(2,1)}) %all-gather.16.cloned.1.call-update) | async-done | bytes 16777232 | tf_op jit(solution)/shard_map/all_gather | solution.py:64
  515.3 52.6 %all-gather.14.cloned.1.call-done = bf16[512,4096]{0,1:T(8,128)(2,1)} async-done(((bf16[512,1024]{0,1:T(8,128)(2,1)}), bf16[512,4096]{0,1:T(8,128)(2,1)}) %all-gather.14.cloned.1.call-update) | async-done | bytes 4194320 | tf_op jit(solution)/shard_map/all_gather | solution.py:66
  568.0 13.6 %fusion.11 = bf16[1,512,2048]{2,1,0:T(8,128)(2,1)S(1)} fusion(bf16[512,4096]{0,1:T(8,128)(2,1)} %all-gather.14.cloned.1.call-done, bf16[4096,2048]{1,0:T(8,128)(2,1)} %all-gather.16.cloned.1.call-done), kind=kOutput, calls=%fused_computation.22 | convolution fusion | flops 8590983168 | bytes 23068672 | tf_op jit(solution)/shard_map/dot_general | solution.py:65
  581.6 5.2 copy.40
  586.8 14.5 %reduce.3 = bf16[512,2048]{1,0:T(8,128)(2,1)} reduce(bf16[512,1,2048]{2,1,0:T(2,128)(2,1)} %bitcast.54, bf16[]{:T(256)} %broadcast.27), dimensions={1}, to_apply=%bitcast.44.reduce_sub_computation | reduce | bytes 4194306
  601.3 4.5 reshape.56
  605.8 29.9 %all_to_all.25 = bf16[4,2,131072]{2,1,0:T(2,128)(2,1)} all-to-all(bf16[4,2,131072]{2,1,0:T(2,128)(2,1)} %reshape.56), channel_id=1, replica_groups=mesh['seq'=4,'fsdp'=8] {'seq'}, dimensions={0} | all-to-all | bytes 4194304 | tf_op jit(solution)/shard_map/all_to_all | solution.py:71
  635.7 4.9 reshape.57
  640.7 6.8 %copy.39 = f32[1,4,128,2048]{3,1,2,0:T(4,128)} copy(bf16[1,4,128,2048]{3,0,2,1:T(2,128)(2,1)} %bitcast.56) | data formatting | bytes 6291456 | tf_op jit(solution)/shard_map/convert_element_type | solution.py:72
  647.5 6.0 reshape.51
  653.5 4.6 convert_add_fusion
  (35 shorter events, 1.3 us)
Async XLA Ops:
  6.5 2.3 copy-start
  6.5 109.4 %all-gather.12.cloned.1.call-start = ((), (), s32[]{:S(2)}) async-start(), calls=%async_computation.6 | async-start | bytes 2359296 | tf_op jit(solution)/shard_map/all_gather | solution.py:30
  7.3 113.0 %all-gather.10.cloned.1.call-start = ((), (), s32[]{:S(2)}) async-start(), calls=%async_computation.5 | async-start | bytes 2359296 | tf_op jit(solution)/shard_map/all_gather | solution.py:29
  8.0 1.3 copy-start.2
  8.0 215.1 %all-gather.8.cloned.1.call-start = ((), (), s32[]{:S(2)}) async-start(), calls=%async_computation.3 | async-start | bytes 18874368 | tf_op jit(solution)/shard_map/all_gather | solution.py:28
  8.8 260.8 %all-reduce.2.cloned.1.call-start = ((), (), s32[]{:S(2)}) async-start(), calls=%async_computation.7 | async-start | bytes 1048576 | tf_op jit(solution)/shard_map/psum | solution.py:40
  120.2 186.2 %all-gather.18.cloned.1.call-start = ((), (), s32[]{:S(2)}) async-start(), calls=%async_computation.10 | async-start | bytes 2621440 | tf_op jit(solution)/shard_map/all_gather | solution.py:10
  124.7 237.2 %reduce-scatter.2.cloned.1.call-start = ((), (), s32[]{:S(2)}) async-start(), calls=%async_computation.4 | async-start | bytes 5242880 | tf_op jit(solution)/shard_map/reduce_scatter | solution.py:35
  237.5 277.9 %all-gather.16.cloned.1.call-start = ((), (), s32[]{:S(2)}) async-start(), calls=%async_computation.9 | async-start | bytes 18874368 | tf_op jit(solution)/shard_map/all_gather | solution.py:64
  238.2 329.7 %all-gather.14.cloned.1.call-start = ((), (), s32[]{:S(2)}) async-start(), calls=%async_computation.8 | async-start | bytes 5242880 | tf_op jit(solution)/shard_map/all_gather | solution.py:66
  380.7 1.0 copy-start.1
Sparse Core Ops, SparseCore 0:
  8.9 31.8 all-gather.11
  42.4 28.5 all-gather.9
  72.6 150.4 all-gather.7
  226.0 43.5 all-reduce.1
  271.3 35.1 all-gather.17
  309.3 52.5 reduce-scatter.1
  363.5 151.7 all-gather.15
  517.2 50.7 all-gather.13
